TPU v7x, 32 devices: a whole 2x2x4 slice. The times are simulated.
32 devices in a mesh: row: 8 (over z, core), col: 4 (over y, x).
Axes of the slice: x: 2, y: 2, z: 4, core: 2. Of those that a mesh axis runs over, the one named last changes fastest.
Arguments:
- u_start: float32 [128, 131072], P('col', 'row'), may hold values from -24 to 24
- v_start: float32 [128, 65536], P('row', 'col'), may hold values from -24 to 24
- keep_u: float32 [128, 40], replicated, may hold values from -1 to 1, as said below
- keep_v: float32 [128, 40], replicated, may hold values from -1 to 1, as said below
- v_next: float32 [65536], P(('col', 'row')), may hold values from -96 to 96
- tile_blocks: bfloat16 [2048, 256, 256], P(('row', 'col')), may hold values from -0.375 to 0.375
- tile_rows: int32 [2048], P(('row', 'col')), may hold values from 0 to 63
- tile_cols: int32 [2048], P(('row', 'col')), may hold values from 0 to 63
- tile_count: int32 [32], P(('row', 'col')), may hold values from 32 to 64
Outputs:
- u_basis: float32 [42, 131072], P(None, ('row', 'col'))
- v_basis: float32 [43, 65536], P(None, ('col', 'row'))
- bidiagonal: float32 [2, 2], replicated
Inputs may be any that keep to these rules, and one draw needn't show every extreme that they name: `tile_rows`: tile row within the device's row group. `tile_cols`: tile column within the device's column group. `tile_count`: slots at this index and beyond hold no tile. `keep_u`: the columns are orthonormal. `keep_v`: the columns are orthonormal.
All inputs are finite; a program needn't handle non-finite values.
Results may differ from a plain program's by a relative error of at most 0.00155.
Values may be sent and summed in bfloat16 or wider, within the bound.
A program may use at most 64 MiB of HBM per device.

v0:
```python
import jax
import jax.numpy as jnp
from jax import lax
from jax.sharding import PartitionSpec as P

STEPS = 2
HIGH = lax.Precision.HIGHEST


def orthonormal(basis_rows, vector, length, gram_matrix):
    first_coef = lax.psum(jnp.dot(basis_rows, vector, precision=HIGH), ("row", "col")) / length
    once_clean = vector - jnp.dot(first_coef, basis_rows, precision=HIGH)
    second_coef, mean_square = lax.psum(
        (jnp.dot(basis_rows, once_clean, precision=HIGH), jnp.sum(once_clean * once_clean)),
        ("row", "col"),
    )
    second_coef = second_coef / length
    gram_coef = jnp.dot(gram_matrix, second_coef, precision=HIGH)
    mean_square = (
        mean_square / length
        - 2.0 * jnp.dot(second_coef, second_coef, precision=HIGH)
        + jnp.dot(second_coef, gram_coef, precision=HIGH)
    )
    twice_clean = once_clean - jnp.dot(second_coef, basis_rows, precision=HIGH)
    scale_now = jnp.sqrt(mean_square + 1e-06)
    cross_terms = (second_coef - gram_coef) / scale_now
    corner = mean_square / (scale_now * scale_now)
    upper_part = jnp.concatenate([gram_matrix, cross_terms[:, None]], axis=1)
    bottom = jnp.concatenate([cross_terms, corner[None]])[None, :]
    grown = jnp.concatenate([upper_part, bottom], axis=0)
    return (twice_clean / scale_now, scale_now, grown)


def per_device(
    u_start, v_start, keep_u, keep_v, v_next, tile_blocks, tile_rows, tile_cols, tile_count
):
    row_total = lax.axis_size("row")
    col_total = lax.axis_size("col")
    u_here = u_start.shape[0]
    u_part = lax.dynamic_slice_in_dim(keep_u, lax.axis_index("col") * u_here, u_here, 0)
    u_kept = lax.psum_scatter(
        jnp.dot(u_part.T, u_start, precision=HIGH), "col", scatter_dimension=1, tiled=True
    )
    v_here = v_start.shape[0]
    v_part = lax.dynamic_slice_in_dim(keep_v, lax.axis_index("row") * v_here, v_here, 0)
    v_kept = lax.psum_scatter(
        jnp.dot(v_part.T, v_start, precision=HIGH), "row", scatter_dimension=1, tiled=True
    )
    u_length = u_kept.shape[1] * row_total * col_total
    v_length = v_kept.shape[1] * row_total * col_total
    gram_left, gram_right = lax.psum(
        (jnp.dot(u_kept, u_kept.T, precision=HIGH), jnp.dot(v_kept, v_kept.T, precision=HIGH)),
        ("row", "col"),
    )
    gram_left = gram_left / u_length
    gram_right = gram_right / v_length
    tile_size = tile_blocks.shape[1]
    slot_total = tile_blocks.shape[0]
    row_blocks = u_kept.shape[1] * col_total // tile_size
    col_blocks = v_kept.shape[1] * row_total // tile_size
    active = (jnp.arange(slot_total, dtype=jnp.int32) < tile_count[0]).astype(jnp.float32)
    row_hot = (tile_rows[None, :] == jnp.arange(row_blocks, dtype=jnp.int32)[:, None]).astype(
        jnp.float32
    ) * active[None, :]
    col_hot = (tile_cols[None, :] == jnp.arange(col_blocks, dtype=jnp.int32)[:, None]).astype(
        jnp.float32
    ) * active[None, :]
    first_right, beta_start, gram_right = orthonormal(v_kept, v_next, v_length, gram_right)
    left_rows = u_kept
    right_rows = jnp.concatenate([v_kept, first_right[None, :]], axis=0)
    current = first_right
    alpha_list = []
    beta_list = []
    for iteration in range(STEPS):
        forward_gathered = lax.all_gather(current.astype(jnp.bfloat16), "row", axis=0, tiled=True)
        forward_picked = forward_gathered.reshape(col_blocks, tile_size)[tile_cols]
        forward_products = jnp.einsum(
            "tij,tj->ti", tile_blocks, forward_picked, preferred_element_type=jnp.float32
        )
        forward_partial_value = jnp.dot(row_hot, forward_products, precision=HIGH).reshape(-1)
        image = lax.psum_scatter(forward_partial_value, "col", scatter_dimension=0, tiled=True)
        left_new, alpha, gram_left = orthonormal(left_rows, image, u_length, gram_left)
        left_rows = jnp.concatenate([left_rows, left_new[None, :]], axis=0)
        gathered = lax.all_gather(left_new.astype(jnp.bfloat16), "col", axis=0, tiled=True)
        picked = gathered.reshape(row_blocks, tile_size)[tile_rows]
        products = jnp.einsum("tij,ti->tj", tile_blocks, picked, preferred_element_type=jnp.float32)
        partial_value = jnp.dot(col_hot, products, precision=HIGH).reshape(-1)
        back_image = lax.psum_scatter(partial_value, "row", scatter_dimension=0, tiled=True)
        current, beta, gram_right = orthonormal(right_rows, back_image, v_length, gram_right)
        right_rows = jnp.concatenate([right_rows, current[None, :]], axis=0)
        alpha_list.append(alpha)
        beta_list.append(beta)
    bidiagonal = jnp.stack([jnp.stack(alpha_list), jnp.stack(beta_list)])
    return (left_rows, right_rows, bidiagonal)


def solution(mesh):
    return jax.shard_map(
        per_device,
        mesh=mesh,
        in_specs=(
            P("col", "row"),
            P("row", "col"),
            P(),
            P(),
            P(("col", "row")),
            P(("row", "col"), None, None),
            P(("row", "col")),
            P(("row", "col")),
            P(("row", "col")),
        ),
        out_specs=(P(None, ("row", "col")), P(None, ("col", "row")), P()),
        check_vma=False,
    )
```

profile of v0, /device:TPU:0, one launch (start us, length us, event | category | flops | bytes accessed | tf_op | source)
XLA Modules:
  0.0 769.2 jit_solution(18316599006986476255)
XLA Ops:
  7.3 5.1 fusion.49
  12.5 4.5 fusion.51
  20.3 32.9 %reduce-scatter.5.cloned.1.call-done = f32[40,2048]{1,0:T(8,128)} async-done(((f32[40,16384]{1,0:T(8,128)}), f32[40,2048]{1,0:T(8,128)}) %reduce-scatter.5.cloned.1.call-update) | async-done | bytes 327696 | tf_op jit(solution)/shard_map/reduce_scatter | solution.py:46
  54.5 38.4 %psum.119 = f32[40]{0:T(128)S(1)} all-reduce(f32[40]{0:T(128)S(1)} %convolution_bitcast_fusion.18), channel_id=1, replica_groups=mesh['row'=8,'col'=4] {'row','col'}, use_global_device_ids=true, to_apply=%region_2.0 | all-reduce | flops 40 | bytes 320 | tf_op jit(solution)/shard_map/psum | solution.py:11
  96.0 1.6 fusion.128
  97.6 42.2 %all-reduce.8 = (f32[40]{0:T(128)S(1)}, f32[]{:T(128)}, f32[40,40]{1,0:T(8,128)S(1)}) all-reduce(f32[40]{0:T(128)S(1)} %convolution_bitcast_fusion.17, f32[]{:T(128)} %get-tuple-element.37, f32[40,40]{1,0:T(8,128)S(1)} %fusion.128), channel_id=1, replica_groups=mesh['row'=8,'col'=4] {'row','col'}, use_global_device_ids=true, to_apply=%region_3.0 | all-reduce | flops 1641 | bytes 13128 | tf_op jit(solution)/shard_map/psum | solution.py:13
  143.9 14.1 %all_gather.12 = bf16[16384]{0:T(1024)(128)(2,1)S(1)} all-gather(bf16[2048]{0:T(1024)(128)(2,1)S(1)} %get-tuple-element.35), channel_id=1, replica_groups=mesh['row'=8,'col'=4] {'row'}, dimensions={0}, use_global_device_ids=true | all-gather | bytes 36864 | tf_op jit(solution)/shard_map/all_gather | solution.py:75
  158.7 5.6 fusion.24
  165.5 1.9 fusion.129
  167.5 39.4 %all-reduce.14.cloned.1.call-done = f32[16384]{0:T(1024)} async-done(((f32[16384]{0:T(1024)}), f32[16384]{0:T(1024)}) %all-reduce.14.cloned.1.call-update) | async-done | bytes 65552
  207.6 1.7 convolution_bitcast_fusion.11
  209.3 39.4 %psum.123 = f32[40]{0:T(128)S(1)} all-reduce(f32[40]{0:T(128)S(1)} %convolution_bitcast_fusion.11), channel_id=1, replica_groups=mesh['row'=8,'col'=4] {'row','col'}, use_global_device_ids=true, to_apply=%region_8.0 | all-reduce | flops 40 | bytes 320 | tf_op jit(solution)/shard_map/psum | solution.py:11
  248.7 1.5 fusion.77
  251.5 1.7 convolution_bitcast_fusion.10
  253.2 41.4 %all-reduce.7 = (f32[40]{0:T(128)S(1)}, f32[]{:T(128)}, f32[40,40]{1,0:T(8,128)S(1)}) all-reduce(f32[40]{0:T(128)S(1)} %convolution_bitcast_fusion.10, f32[]{:T(128)} %get-tuple-element.33, f32[40,40]{1,0:T(8,128)S(1)} %fusion.129), channel_id=1, replica_groups=mesh['row'=8,'col'=4] {'row','col'}, use_global_device_ids=true, to_apply=%region_9.0 | all-reduce | flops 1641 | bytes 13128 | tf_op jit(solution)/shard_map/psum | solution.py:13
  297.4 1.5 fusion.75
  298.9 8.9 %all_gather.13 = bf16[16384]{0:T(1024)(128)(2,1)S(1)} all-gather(bf16[4096]{0:T(1024)(128)(2,1)S(1)} %get-tuple-element.31), channel_id=1, replica_groups=mesh['row'=8,'col'=4] {'col'}, dimensions={0}, use_global_device_ids=true | all-gather | bytes 40960 | tf_op jit(solution)/shard_map/all_gather | solution.py:84
  308.6 4.6 fusion.21
  314.4 53.6 %all-reduce.16.cloned.1.call-done = f32[16384]{0:T(1024)} async-done(((f32[16384]{0:T(1024)}), f32[16384]{0:T(1024)}) %all-reduce.16.cloned.1.call-update) | async-done | bytes 65552
  369.1 39.2 %psum.127 = f32[41]{0:T(128)S(1)} all-reduce(f32[41]{0:T(128)S(1)} %convolution_bitcast_fusion.16), channel_id=1, replica_groups=mesh['row'=8,'col'=4] {'row','col'}, use_global_device_ids=true, to_apply=%region_14.0 | all-reduce | flops 41 | bytes 328 | tf_op jit(solution)/shard_map/psum | solution.py:11
  410.3 40.0 %all-reduce.6 = (f32[41]{0:T(128)S(1)}, f32[]{:T(128)}) all-reduce(f32[41]{0:T(128)S(1)} %convolution_bitcast_fusion.15, f32[]{:T(128)} %get-tuple-element.29), channel_id=1, replica_groups=mesh['row'=8,'col'=4] {'row','col'}, use_global_device_ids=true, to_apply=%region_15.0 | all-reduce | flops 42 | bytes 336 | tf_op jit(solution)/shard_map/psum | solution.py:13
  453.5 14.1 %all_gather.14 = bf16[16384]{0:T(1024)(128)(2,1)S(1)} all-gather(bf16[2048]{0:T(1024)(128)(2,1)S(1)} %get-tuple-element.27), channel_id=1, replica_groups=mesh['row'=8,'col'=4] {'row'}, dimensions={0}, use_global_device_ids=true | all-gather | bytes 36864 | tf_op jit(solution)/shard_map/all_gather | solution.py:75
  468.4 5.6 fusion.18
  475.2 41.8 %all-reduce.18.cloned.1.call-done = f32[16384]{0:T(1024)} async-done(((f32[16384]{0:T(1024)}), f32[16384]{0:T(1024)}) %all-reduce.18.cloned.1.call-update) | async-done | bytes 65552
  518.4 39.2 %psum.130 = f32[41]{0:T(128)S(1)} all-reduce(f32[41]{0:T(128)S(1)} %convolution_bitcast_fusion.7), channel_id=1, replica_groups=mesh['row'=8,'col'=4] {'row','col'}, use_global_device_ids=true, to_apply=%region_19.0 | all-reduce | flops 41 | bytes 328 | tf_op jit(solution)/shard_map/psum | solution.py:11
  558.2 1.3 multiply_reduce_fusion
  560.2 41.4 %all-reduce.5 = (f32[41]{0:T(128)S(1)}, f32[]{:T(128)}) all-reduce(f32[41]{0:T(128)S(1)} %convolution_bitcast_fusion.6, f32[]{:T(128)} %get-tuple-element.25), channel_id=1, replica_groups=mesh['row'=8,'col'=4] {'row','col'}, use_global_device_ids=true, to_apply=%region_20.0 | all-reduce | flops 42 | bytes 336 | tf_op jit(solution)/shard_map/psum | solution.py:13
  605.6 9.1 %all_gather.15 = bf16[16384]{0:T(1024)(128)(2,1)S(1)} all-gather(bf16[4096]{0:T(1024)(128)(2,1)S(1)} %get-tuple-element.23), channel_id=1, replica_groups=mesh['row'=8,'col'=4] {'col'}, dimensions={0}, use_global_device_ids=true | all-gather | bytes 40960 | tf_op jit(solution)/shard_map/all_gather | solution.py:84
  615.4 4.6 fusion.15
  621.9 52.8 %all-reduce.20.cloned.1.call-done = f32[16384]{0:T(1024)} async-done(((f32[16384]{0:T(1024)}), f32[16384]{0:T(1024)}) %all-reduce.20.cloned.1.call-update) | async-done | bytes 65552
  675.8 39.3 %psum.133 = f32[42]{0:T(128)S(1)} all-reduce(f32[42]{0:T(128)S(1)} %convolution_bitcast_fusion.14), channel_id=1, replica_groups=mesh['row'=8,'col'=4] {'row','col'}, use_global_device_ids=true, to_apply=%region_24.0 | all-reduce | flops 42 | bytes 336 | tf_op jit(solution)/shard_map/psum | solution.py:11
  717.1 40.0 %all-reduce.4 = (f32[42]{0:T(128)S(1)}, f32[]{:T(128)}) all-reduce(f32[42]{0:T(128)S(1)} %convolution_bitcast_fusion.13, f32[]{:T(128)} %get-tuple-element.21), channel_id=1, replica_groups=mesh['row'=8,'col'=4] {'row','col'}, use_global_device_ids=true, to_apply=%region_25.0 | all-reduce | flops 43 | bytes 344 | tf_op jit(solution)/shard_map/psum | solution.py:13
  (104 shorter events, 34.0 us)
Async XLA Ops:
  7.2 5.3 copy-start
  7.2 10.6 %copy-start.7 = (u32[32]{0:T(128)S(1)}, u32[32]{0:T(128)}, u32[]{:S(2)}) copy-start(u32[32]{0:T(128)} %constant.69) | copy-start | bytes 388
  7.2 11.1 %copy-start.6 = (u32[32]{0:T(128)S(1)}, u32[32]{0:T(128)}, u32[]{:S(2)}) copy-start(u32[32]{0:T(128)} %constant.73) | copy-start | bytes 388
  7.2 13.0 %copy-start.5 = (s32[64]{0:T(128)S(1)}, s32[64]{0:T(128)}, u32[]{:S(2)}) copy-start(s32[64]{0:T(128)} %param.16) | copy-start | bytes 772
  7.2 13.1 %copy-start.4 = (s32[64]{0:T(128)S(1)}, s32[64]{0:T(128)}, u32[]{:S(2)}) copy-start(s32[64]{0:T(128)} %param.15) | copy-start | bytes 772
  7.2 46.0 %copy-start.3 = (f32[2048]{0:T(1024)S(1)}, f32[2048]{0:T(1024)}, u32[]{:S(2)}) copy-start(f32[2048]{0:T(1024)} %param.13) | copy-start | bytes 24580
  7.2 45.9 %reduce-scatter.5.cloned.1.call-start = ((), (), s32[]{:S(2)}) async-start(), calls=%async_computation.3 | async-start | bytes 2949120 | tf_op jit(solution)/shard_map/reduce_scatter | solution.py:46
  12.5 153.0 %reduce-scatter.3.cloned.1.call-start = ((), (), s32[]{:S(2)}) async-start(), calls=%async_computation.2 | async-start | bytes 3276800 | tf_op jit(solution)/shard_map/reduce_scatter | solution.py:41
  17.0 189.8 %all-reduce.14.cloned.1.call-start = ((), (), s32[]{:S(2)}) async-start(), calls=%async_computation.4 | async-start | bytes 131072
  165.4 202.6 %all-reduce.16.cloned.1.call-start = ((), (), s32[]{:S(2)}) async-start(), calls=%async_computation.5 | async-start | bytes 131072
  308.6 60.1 %copy-start.2 = (f32[40,2048]{1,0:T(8,128)S(1)}, f32[40,2048]{1,0:T(8,128)}, u32[]{:S(2)}) copy-start(f32[40,2048]{1,0:T(8,128)} %reduce-scatter.5.cloned.1.call-done) | copy-start | bytes 983044
  313.2 204.5 %copy-start.1 = (f32[40,4096]{1,0:T(8,128)S(1)}, f32[40,4096]{1,0:T(8,128)}, u32[]{:S(2)}) copy-start(f32[40,4096]{1,0:T(8,128)} %reduce-scatter.3.cloned.1.call-done) | copy-start | bytes 1966084
  314.1 202.9 %all-reduce.18.cloned.1.call-start = ((), (), s32[]{:S(2)}) async-start(), calls=%async_computation.6 | async-start | bytes 131072
  474.9 199.8 %all-reduce.20.cloned.1.call-start = ((), (), s32[]{:S(2)}) async-start(), calls=%async_computation.7 | async-start | bytes 131072
Sparse Core Ops, SparseCore 0:
  12.6 40.5 reduce-scatter.4
  56.2 39.4 reduce-scatter.2
  165.5 41.3 all-reduce.13
  314.2 53.6 all-reduce.15
  475.0 41.9 all-reduce.17
  621.0 53.6 all-reduce.19
where the time goes:
time: 772 us; the launch traced here: 769 us
  blocking collectives  447 us (58%)
  waiting for transfers between devices  221 us (29%)
  matrix products  55.3 us (7%)
  between operations  26.5 us (3%)
  other arithmetic  9.86 us (1%)
  local copies, waits for them, and re-layouts  9.85 us (1%)
    psum x5, blocking collectives, orthonormal(): lax.psum((jnp.dot(basis_rows, once_clean, precision=HIGH), jnp.sum(once_c...  205 us
    psum x5, blocking collectives, orthonormal(): lax.psum(jnp.dot(basis_rows, vector, precision=HIGH), ('row', 'col'))  196 us
    unnamed x10, waiting for transfers between devices  188 us
    reduce_scatter x1, waiting for transfers between devices, per_device(): lax.psum_scatter(jnp.dot(v_part.T, v_start, precision=HIGH), 'row', scatt...  32.9 us
    all_gather x2, blocking collectives, per_device(): lax.all_gather(current.astype(jnp.bfloat16), 'row', axis=0, tiled=True)  28.2 us
    all_gather x2, blocking collectives, per_device(): lax.all_gather(left_new.astype(jnp.bfloat16), 'col', axis=0, tiled=True)  18.1 us
  transfers between devices with their start and end apart: 6, of which 5 were waited for; matrix products, arithmetic and copies ran while one was open for 3% of the time, Pallas kernels for 0%

commit v1 on v0

--- a/solution.py
+++ b/solution.py
@@ -8,7 +8,10 @@
 
 
 def orthonormal(basis_rows, vector, length, gram_matrix):
-    first_coef = lax.psum(jnp.dot(basis_rows, vector, precision=HIGH), ("row", "col")) / length
+    first_coef = (
+        jnp.sum(lax.all_gather(jnp.dot(basis_rows, vector, precision=HIGH), ("row", "col")), axis=0)
+        / length
+    )
     once_clean = vector - jnp.dot(first_coef, basis_rows, precision=HIGH)
     second_coef, mean_square = lax.psum(
         (jnp.dot(basis_rows, once_clean, precision=HIGH), jnp.sum(once_clean * once_clean)),

time: 772 us -> 774 us (level)
    unnamed x0 -> x5, blocking collectives: none -> 196 us
    psum x5 -> x0, blocking collectives: 196 us -> none  [orthonormal(): lax.psum(jnp.dot(basis_rows, vector, precision=HIGH), ('row', 'col'))]
where the time goes in v1:
time: 774 us; the launch traced here: 771 us
  blocking collectives  447 us (58%)
  waiting for transfers between devices  221 us (29%)
  matrix products  55.3 us (7%)
  between operations  26.5 us (3%)
  local copies, waits for them, and re-layouts  11.4 us (1%)
  other arithmetic  9.98 us (1%)
    psum x5, blocking collectives, orthonormal(): lax.psum((jnp.dot(basis_rows, once_clean, precision=HIGH), jnp.sum(once_c...  205 us
    unnamed x5, blocking collectives  196 us
    unnamed x10, waiting for transfers between devices  188 us
    reduce_scatter x1, waiting for transfers between devices, per_device(): lax.psum_scatter(jnp.dot(v_part.T, v_start, precision=HIGH), 'row', scatt...  32.9 us
    all_gather x2, blocking collectives, per_device(): lax.all_gather(current.astype(jnp.bfloat16), 'row', axis=0, tiled=True)  28.2 us
    all_gather x2, blocking collectives, per_device(): lax.all_gather(left_new.astype(jnp.bfloat16), 'col', axis=0, tiled=True)  18.1 us
  transfers between devices with their start and end apart: 6, of which 5 were waited for; matrix products, arithmetic and copies ran while one was open for 3% of the time, Pallas kernels for 0%

profile of v1, /device:TPU:0, one launch (start us, length us, event | category | flops | bytes accessed | tf_op | source)
XLA Modules:
  0.0 771.5 jit_solution(1003190782267350119)
XLA Ops:
  7.3 5.1 fusion.49
  12.5 4.5 fusion.51
  20.3 32.9 %reduce-scatter.5.cloned.1.call-done = f32[40,2048]{1,0:T(8,128)} async-done(((f32[40,16384]{1,0:T(8,128)}), f32[40,2048]{1,0:T(8,128)}) %reduce-scatter.5.cloned.1.call-update) | async-done | bytes 327696 | tf_op jit(solution)/shard_map/reduce_scatter | solution.py:49
  54.7 38.3 %all-reduce = f32[1280]{0:T(1024)S(1)} all-reduce(f32[1280]{0:T(1024)S(1)} %dynamic-update-slice), channel_id=2, replica_groups=mesh['row'=8,'col'=4] {'row','col'}, use_global_device_ids=true, to_apply=%add | all-reduce | flops 1280 | bytes 10240
  96.3 1.6 fusion.128
  97.9 42.2 %all-reduce.13 = (f32[40]{0:T(128)S(1)}, f32[]{:T(128)}, f32[40,40]{1,0:T(8,128)S(1)}) all-reduce(f32[40]{0:T(128)S(1)} %convolution_bitcast_fusion.17, f32[]{:T(128)} %get-tuple-element.37, f32[40,40]{1,0:T(8,128)S(1)} %fusion.128), channel_id=1, replica_groups=mesh['row'=8,'col'=4] {'row','col'}, use_global_device_ids=true, to_apply=%region_3.0 | all-reduce | flops 1641 | bytes 13128 | tf_op jit(solution)/shard_map/psum | solution.py:16
  144.1 14.1 %all_gather.44 = bf16[16384]{0:T(1024)(128)(2,1)S(1)} all-gather(bf16[2048]{0:T(1024)(128)(2,1)S(1)} %get-tuple-element.35), channel_id=1, replica_groups=mesh['row'=8,'col'=4] {'row'}, dimensions={0}, use_global_device_ids=true | all-gather | bytes 36864 | tf_op jit(solution)/shard_map/all_gather | solution.py:78
  158.9 5.6 fusion.24
  165.7 1.9 fusion.129
  167.7 39.6 %all-reduce.19.cloned.1.call-done = f32[16384]{0:T(1024)} async-done(((f32[16384]{0:T(1024)}), f32[16384]{0:T(1024)}) %all-reduce.19.cloned.1.call-update) | async-done | bytes 65552
  208.0 1.7 convolution_bitcast_fusion.11
  209.9 39.5 %all-reduce.1 = f32[1280]{0:T(1024)S(1)} all-reduce(f32[1280]{0:T(1024)S(1)} %dynamic-update-slice.1), channel_id=3, replica_groups=mesh['row'=8,'col'=4] {'row','col'}, use_global_device_ids=true, to_apply=%add.1 | all-reduce | flops 1280 | bytes 10240
  249.6 1.5 fusion.77
  252.4 1.7 convolution_bitcast_fusion.10
  254.1 41.4 %all-reduce.12 = (f32[40]{0:T(128)S(1)}, f32[]{:T(128)}, f32[40,40]{1,0:T(8,128)S(1)}) all-reduce(f32[40]{0:T(128)S(1)} %convolution_bitcast_fusion.10, f32[]{:T(128)} %get-tuple-element.33, f32[40,40]{1,0:T(8,128)S(1)} %fusion.129), channel_id=1, replica_groups=mesh['row'=8,'col'=4] {'row','col'}, use_global_device_ids=true, to_apply=%region_9.0 | all-reduce | flops 1641 | bytes 13128 | tf_op jit(solution)/shard_map/psum | solution.py:16
  298.3 1.5 fusion.75
  299.8 8.9 %all_gather.47 = bf16[16384]{0:T(1024)(128)(2,1)S(1)} all-gather(bf16[4096]{0:T(1024)(128)(2,1)S(1)} %get-tuple-element.31), channel_id=1, replica_groups=mesh['row'=8,'col'=4] {'col'}, dimensions={0}, use_global_device_ids=true | all-gather | bytes 40960 | tf_op jit(solution)/shard_map/all_gather | solution.py:87
  309.5 4.6 fusion.21
  315.3 53.6 %all-reduce.21.cloned.1.call-done = f32[16384]{0:T(1024)} async-done(((f32[16384]{0:T(1024)}), f32[16384]{0:T(1024)}) %all-reduce.21.cloned.1.call-update) | async-done | bytes 65552
  370.2 39.3 %all-reduce.2 = f32[1312]{0:T(1024)S(1)} all-reduce(f32[1312]{0:T(1024)S(1)} %dynamic-update-slice.2), channel_id=4, replica_groups=mesh['row'=8,'col'=4] {'row','col'}, use_global_device_ids=true, to_apply=%add.2 | all-reduce | flops 1312 | bytes 10496
  411.7 40.0 %all-reduce.11 = (f32[41]{0:T(128)S(1)}, f32[]{:T(128)}) all-reduce(f32[41]{0:T(128)S(1)} %convolution_bitcast_fusion.15, f32[]{:T(128)} %get-tuple-element.29), channel_id=1, replica_groups=mesh['row'=8,'col'=4] {'row','col'}, use_global_device_ids=true, to_apply=%region_15.0 | all-reduce | flops 42 | bytes 336 | tf_op jit(solution)/shard_map/psum | solution.py:16
  454.9 14.1 %all_gather.50 = bf16[16384]{0:T(1024)(128)(2,1)S(1)} all-gather(bf16[2048]{0:T(1024)(128)(2,1)S(1)} %get-tuple-element.27), channel_id=1, replica_groups=mesh['row'=8,'col'=4] {'row'}, dimensions={0}, use_global_device_ids=true | all-gather | bytes 36864 | tf_op jit(solution)/shard_map/all_gather | solution.py:78
  469.7 5.6 fusion.18
  476.5 41.8 %all-reduce.23.cloned.1.call-done = f32[16384]{0:T(1024)} async-done(((f32[16384]{0:T(1024)}), f32[16384]{0:T(1024)}) %all-reduce.23.cloned.1.call-update) | async-done | bytes 65552
  520.0 39.6 %all-reduce.3 = f32[1312]{0:T(1024)S(1)} all-reduce(f32[1312]{0:T(1024)S(1)} %dynamic-update-slice.3), channel_id=5, replica_groups=mesh['row'=8,'col'=4] {'row','col'}, use_global_device_ids=true, to_apply=%add.3 | all-reduce | flops 1312 | bytes 10496
  560.2 1.3 multiply_reduce_fusion
  562.2 41.2 %all-reduce.10 = (f32[41]{0:T(128)S(1)}, f32[]{:T(128)}) all-reduce(f32[41]{0:T(128)S(1)} %convolution_bitcast_fusion.6, f32[]{:T(128)} %get-tuple-element.25), channel_id=1, replica_groups=mesh['row'=8,'col'=4] {'row','col'}, use_global_device_ids=true, to_apply=%region_20.0 | all-reduce | flops 42 | bytes 336 | tf_op jit(solution)/shard_map/psum | solution.py:16
  607.3 9.1 %all_gather.53 = bf16[16384]{0:T(1024)(128)(2,1)S(1)} all-gather(bf16[4096]{0:T(1024)(128)(2,1)S(1)} %get-tuple-element.23), channel_id=1, replica_groups=mesh['row'=8,'col'=4] {'col'}, dimensions={0}, use_global_device_ids=true | all-gather | bytes 40960 | tf_op jit(solution)/shard_map/all_gather | solution.py:87
  617.2 4.6 fusion.15
  623.7 52.9 %all-reduce.25.cloned.1.call-done = f32[16384]{0:T(1024)} async-done(((f32[16384]{0:T(1024)}), f32[16384]{0:T(1024)}) %all-reduce.25.cloned.1.call-update) | async-done | bytes 65552
  677.9 39.3 %all-reduce.4 = f32[1344]{0:T(1024)S(1)} all-reduce(f32[1344]{0:T(1024)S(1)} %dynamic-update-slice.4), channel_id=6, replica_groups=mesh['row'=8,'col'=4] {'row','col'}, use_global_device_ids=true, to_apply=%add.4 | all-reduce | flops 1344 | bytes 10752
  719.4 40.0 %all-reduce.9 = (f32[42]{0:T(128)S(1)}, f32[]{:T(128)}) all-reduce(f32[42]{0:T(128)S(1)} %convolution_bitcast_fusion.13, f32[]{:T(128)} %get-tuple-element.21), channel_id=1, replica_groups=mesh['row'=8,'col'=4] {'row','col'}, use_global_device_ids=true, to_apply=%region_25.0 | all-reduce | flops 43 | bytes 344 | tf_op jit(solution)/shard_map/psum | solution.py:16
  (124 shorter events, 35.6 us)
Async XLA Ops:
  7.2 5.3 copy-start
  7.2 10.6 %copy-start.7 = (u32[32]{0:T(128)S(1)}, u32[32]{0:T(128)}, u32[]{:S(2)}) copy-start(u32[32]{0:T(128)} %constant.89) | copy-start | bytes 388
  7.2 11.1 %copy-start.6 = (u32[32]{0:T(128)S(1)}, u32[32]{0:T(128)}, u32[]{:S(2)}) copy-start(u32[32]{0:T(128)} %constant.93) | copy-start | bytes 388
  7.2 13.0 %copy-start.5 = (s32[64]{0:T(128)S(1)}, s32[64]{0:T(128)}, u32[]{:S(2)}) copy-start(s32[64]{0:T(128)} %param.16) | copy-start | bytes 772
  7.2 13.1 %copy-start.4 = (s32[64]{0:T(128)S(1)}, s32[64]{0:T(128)}, u32[]{:S(2)}) copy-start(s32[64]{0:T(128)} %param.15) | copy-start | bytes 772
  7.2 46.0 %copy-start.3 = (f32[2048]{0:T(1024)S(1)}, f32[2048]{0:T(1024)}, u32[]{:S(2)}) copy-start(f32[2048]{0:T(1024)} %param.13) | copy-start | bytes 24580
  7.2 45.9 %reduce-scatter.5.cloned.1.call-start = ((), (), s32[]{:S(2)}) async-start(), calls=%async_computation.3 | async-start | bytes 2949120 | tf_op jit(solution)/shard_map/reduce_scatter | solution.py:49
  12.5 153.2 %reduce-scatter.3.cloned.1.call-start = ((), (), s32[]{:S(2)}) async-start(), calls=%async_computation.2 | async-start | bytes 3276800 | tf_op jit(solution)/shard_map/reduce_scatter | solution.py:44
  17.0 190.3 %all-reduce.19.cloned.1.call-start = ((), (), s32[]{:S(2)}) async-start(), calls=%async_computation.4 | async-start | bytes 131072
  165.6 203.2 %all-reduce.21.cloned.1.call-start = ((), (), s32[]{:S(2)}) async-start(), calls=%async_computation.5 | async-start | bytes 131072
  309.5 60.1 %copy-start.2 = (f32[40,2048]{1,0:T(8,128)S(1)}, f32[40,2048]{1,0:T(8,128)}, u32[]{:S(2)}) copy-start(f32[40,2048]{1,0:T(8,128)} %reduce-scatter.5.cloned.1.call-done) | copy-start | bytes 983044
  314.1 204.9 %copy-start.1 = (f32[40,4096]{1,0:T(8,128)S(1)}, f32[40,4096]{1,0:T(8,128)}, u32[]{:S(2)}) copy-start(f32[40,4096]{1,0:T(8,128)} %reduce-scatter.3.cloned.1.call-done) | copy-start | bytes 1966084
  315.0 203.3 %all-reduce.23.cloned.1.call-start = ((), (), s32[]{:S(2)}) async-start(), calls=%async_computation.6 | async-start | bytes 131072
  476.2 200.3 %all-reduce.25.cloned.1.call-start = ((), (), s32[]{:S(2)}) async-start(), calls=%async_computation.7 | async-start | bytes 131072
Sparse Core Ops, SparseCore 0:
  12.6 40.5 reduce-scatter.4
  56.2 39.3 reduce-scatter.2
  165.7 41.5 all-reduce.18
  315.1 53.6 all-reduce.20
  476.4 41.9 all-reduce.22
  622.8 53.7 all-reduce.24
